TPU v7x, 32 devices: a whole 2x2x4 slice. The times are simulated.
32 devices in a mesh: grp: 8 (over z, x), node: 4 (over y, core).
Axes of the slice: x: 2, y: 2, z: 4, core: 2. Of those that a mesh axis runs over, the one named last changes fastest.
Arguments:
- initial: float32 [6, 32, 32768], P(None, None, ('grp', 'node')), may hold values from -0.5 to 16, as said below
- afferent_noise_level: float32 [32, 32768], P(None, ('grp', 'node')), may hold values from 0.12 to 0.32
- history: bfloat16 [64, 32, 32768], P(None, None, ('grp', 'node')), may hold values from 0 to 1
- weights: bfloat16 [32, 24, 128, 1024], P(('grp', 'node')), may hold values from -0.109375 to 0.109375
- lead_field: bfloat16 [128, 32768], P(None, ('grp', 'node')), may hold values from -0.00390625 to 0.00390625
- src_group: int32 [32, 24], replicated, may hold values from 0 to 7, as said below
- src_sub: int32 [32, 24], replicated, may hold values from 0 to 7
- delays: int32 [32, 24], replicated, may hold values from 6 to 63
- counts: int32 [32], replicated, may hold values from 16 to 24, as said below
Outputs:
- final_state: float32 [6, 32, 32768], P(None, None, ('grp', 'node'))
- sensors: float32 [6, 128, 32], replicated
Inputs may be any that keep to these rules, and one draw needn't show every extreme that they name: `initial`: rows 0 to 2 are potentials and rows 3 to 5 their rates; row 0 lies within 0 and 0.4, row 1 within 4 and 16, row 2 within 0 and 8, rows 3 to 5 within -0.5 and 0.5. `src_group`: among the tiles k < counts[b] of a block b no owner group appears more than 3 times, and some block reaches 3. Tiles k >= counts[b] of block b are ignored; in every draw some block has 24 live tiles.
All inputs are finite; a program needn't handle non-finite values.
Results may differ from a plain program's by a relative error of at most 0.0003.
The roundings to bfloat16 on the way count: a program that leaves them out, or rounds other values in their place, can miss the bound.
Values may be sent and summed in bfloat16 or wider, within the bound.
A program may use at most 128 MiB of HBM per device.

v0:
```python
import jax
import jax.numpy as jnp
from jax import lax
from jax.sharding import PartitionSpec as P

DMIN = 6
STEPS = 6
exciting_amplitude = 3.25
suppressive_amplitude = 22.0
exciting_inverse_lag = 0.1
suppressive_inverse_lag = 0.05
link_factor = 135.0
maximal_spike_frequency = 0.005
thresh = 6.0
fire_slope = 0.56
global_scaling_factor = 0.5
dt_step = 0.5


def sigmoid_spike_density(somatic_charge_level):
    return 1.0 / (1.0 + jnp.exp(fire_slope * (thresh - somatic_charge_level)))


def derivative(population_variables, afferent_noise_level, network_afferent):
    principal_cell_level, interneuron_depolarization, suppressive_depolarization = (
        population_variables[0],
        population_variables[1],
        population_variables[2],
    )
    principal_cell_curvature = (
        exciting_amplitude
        * exciting_inverse_lag
        * maximal_spike_frequency
        * sigmoid_spike_density(interneuron_depolarization - suppressive_depolarization)
        - 2.0 * exciting_inverse_lag * population_variables[3]
        - exciting_inverse_lag * exciting_inverse_lag * principal_cell_level
    )
    interneuron_second_derivative = (
        exciting_amplitude
        * exciting_inverse_lag
        * (
            afferent_noise_level
            + 0.8
            * link_factor
            * maximal_spike_frequency
            * sigmoid_spike_density(link_factor * principal_cell_level)
            + global_scaling_factor * network_afferent
        )
        - 2.0 * exciting_inverse_lag * population_variables[4]
        - exciting_inverse_lag * exciting_inverse_lag * interneuron_depolarization
    )
    suppressive_second_derivative = (
        suppressive_amplitude
        * suppressive_inverse_lag
        * 0.25
        * link_factor
        * maximal_spike_frequency
        * sigmoid_spike_density(0.25 * link_factor * principal_cell_level)
        - 2.0 * suppressive_inverse_lag * population_variables[5]
        - suppressive_inverse_lag * suppressive_inverse_lag * suppressive_depolarization
    )
    return jnp.stack(
        [
            population_variables[3],
            population_variables[4],
            population_variables[5],
            principal_cell_curvature,
            interneuron_second_derivative,
            suppressive_second_derivative,
        ]
    )


def advance(population_variables, afferent_noise_level, coupled_now, coupled_next):
    first_rate = derivative(population_variables, afferent_noise_level, coupled_now)
    second_rate = derivative(
        population_variables + dt_step * first_rate, afferent_noise_level, coupled_next
    )
    return population_variables + 0.5 * dt_step * (first_rate + second_rate)


def body(
    initial, afferent_noise_level, history, weights, lead_field, src_group, src_sub, delays, counts
):
    owners = lax.axis_size("grp")
    columns = lax.axis_size("node")
    my_group = lax.axis_index("grp")
    my_column = lax.axis_index("node")
    myself = my_group * columns + my_column
    cycle_len, replicas, block_len = history.shape
    tiles_max = src_group.shape[1]
    piece_len = weights.shape[2]
    slots_per = (tiles_max + owners - 1) // owners
    zero_index = jnp.zeros((), jnp.int32)
    tile_lanes = jnp.arange(tiles_max, dtype=jnp.int32)
    places = jnp.arange(slots_per, dtype=jnp.int32)
    tile_stack = weights.reshape(tiles_max * piece_len, block_len)

    def column_of(lookup):
        return lax.dynamic_index_in_dim(lookup.reshape(owners, columns, -1), my_column, 1, False)

    col_group = column_of(src_group)
    col_sub = column_of(src_sub)
    col_delay = column_of(delays)
    col_count = column_of(counts)[:, 0]
    matched = (col_group == my_group) & (tile_lanes[None, :] < col_count[:, None])
    ranked = jnp.cumsum(matched.astype(jnp.int32), axis=1) - 1
    picked_slot = matched[:, :, None] & (ranked[:, :, None] == places[None, None, :])
    sel_sub = jnp.sum(jnp.where(picked_slot, col_sub[:, :, None], 0), axis=1)
    sel_delay = jnp.sum(jnp.where(picked_slot, col_delay[:, :, None], 0), axis=1)
    own_group = lax.dynamic_index_in_dim(src_group, myself, 0, False)
    own_count = lax.dynamic_index_in_dim(counts, myself, 0, False)
    own_live = tile_lanes < own_count
    earlier = (
        (own_group[:, None] == own_group[None, :])
        & own_live[None, :]
        & (tile_lanes[None, :] < tile_lanes[:, None])
    )
    own_rank = jnp.minimum(jnp.sum(earlier.astype(jnp.int32), axis=1), slots_per - 1)
    own_mask = own_live.astype(jnp.bfloat16)

    def pack(cycle, in_times):
        how_many = in_times.shape[0]
        slot_ids = jnp.mod(in_times[None, :, None] - sel_delay[:, None, :], cycle_len)
        starts = jnp.broadcast_to(sel_sub[:, None, :] * piece_len, slot_ids.shape)

        def cut_piece(slot_id, start_id):
            return lax.dynamic_slice(
                cycle, (slot_id, zero_index, start_id), (1, replicas, piece_len)
            )[0]

        pieces = jax.vmap(cut_piece)(slot_ids.reshape(-1), starts.reshape(-1))
        return pieces.reshape(owners, how_many, slots_per, replicas, piece_len)

    def unpack(parcel):
        how_many = parcel.shape[1]
        picked = parcel[own_group, :, own_rank] * own_mask[:, None, None, None]
        flattened = jnp.transpose(picked, (1, 2, 0, 3)).reshape(
            how_many * replicas, tiles_max * piece_len
        )
        return jnp.dot(flattened, tile_stack, preferred_element_type=jnp.float32).reshape(
            how_many, replicas, block_len
        )

    def store_fire(cycle, population_variables, step_id):
        spike_density_result = sigmoid_spike_density(
            population_variables[1] - population_variables[2]
        ).astype(jnp.bfloat16)
        return lax.dynamic_update_slice(
            cycle, spike_density_result[None], (jnp.mod(step_id, cycle_len), zero_index, zero_index)
        )

    def record(sensors, population_variables, step_id):
        potential = (population_variables[1] - population_variables[2]).astype(jnp.bfloat16)
        local_sum = lax.dot_general(
            lead_field, potential, (((1,), (1,)), ((), ())), preferred_element_type=jnp.float32
        )
        local_sum = lax.psum(local_sum, ("grp", "node"))
        return lax.dynamic_update_slice(sensors, local_sum[None], (step_id, zero_index, zero_index))

    start_times = jnp.zeros((1,), jnp.int32)
    network_afferent = unpack(
        lax.all_to_all(pack(history, start_times), "grp", split_axis=0, concat_axis=0, tiled=True)
    )[0]
    sensors = jnp.zeros((STEPS, lead_field.shape[0], replicas), jnp.float32)

    def one_batch(batch_id, carried):
        population_variables, cycle, coupled_now, sensors = carried
        base_step = (jnp.asarray(batch_id) * DMIN).astype(jnp.int32)
        cycle = store_fire(cycle, population_variables, base_step)
        in_times = base_step + 1 + jnp.arange(DMIN, dtype=jnp.int32)
        batch_input = unpack(
            lax.all_to_all(pack(cycle, in_times), "grp", split_axis=0, concat_axis=0, tiled=True)
        )
        for offset in range(DMIN):
            step_id = base_step + offset
            if offset > 0:
                cycle = store_fire(cycle, population_variables, step_id)
            population_variables = advance(
                population_variables, afferent_noise_level, coupled_now, batch_input[offset]
            )
            coupled_now = batch_input[offset]
            sensors = record(sensors, population_variables, step_id)
        return (population_variables, cycle, coupled_now, sensors)

    population_variables, cycle, network_afferent, sensors = lax.fori_loop(
        0, STEPS // DMIN, one_batch, (initial, history, network_afferent, sensors)
    )
    return (population_variables, sensors)


def solution(mesh):
    return jax.shard_map(
        body,
        mesh=mesh,
        in_specs=(
            P(None, None, ("grp", "node")),
            P(None, ("grp", "node")),
            P(None, None, ("grp", "node")),
            P(("grp", "node"), None, None, None),
            P(None, ("grp", "node")),
            P(),
            P(),
            P(),
            P(),
        ),
        out_specs=(P(None, None, ("grp", "node")), P()),
        check_vma=False,
    )
```

profile of v0, /device:TPU:8, one launch (start us, length us, event | category | flops | bytes accessed | tf_op | source)
XLA Modules:
  0.0 292.4 jit_solution(6723610397220661307)
XLA Ops:
  7.2 0.8 reshape.515
  8.0 0.8 copy.46
  8.7 0.8 copy.44
  9.5 0.8 copy.43
  11.3 23.1 %copy.48 = bf16[64,32,1024]{1,0,2:T(8,128)(2,1)} copy(bf16[64,32,1024]{2,1,0:T(8,128)(2,1)} %param.11) | data formatting | bytes 8388608 | tf_op args[2]
  34.4 5.5 %gather_fusion = bf16[24,32,128]{1,0,2:T(8,128)(2,1)S(1)} fusion(bf16[64,32,1024]{1,0,2:T(8,128)(2,1)} %copy.48, s32[24]{0:T(128)S(1)} %fusion.184), kind=kCustom, calls=%fused_computation | custom fusion | bytes 393504 | tf_op jit(solution)/shard_map/vmap()/gather | solution.py:128
  39.9 1.1 copy.49
  41.1 6.1 %all-to-all-start = ((bf16[8,1,3,32,128]{4,3,2,1,0:T(8,128)(2,1)}), bf16[8,1,3,32,128]{4,3,2,1,0:T(8,128)(2,1)S(1)}, u32[]{:S(2)}, u32[]{:S(2)}) async-start(bf16[8,1,3,32,128]{4,3,2,1,0:T(8,128)(2,1)} %bitcast.8), calls=%async_computation | async-start | bytes 393216 | tf_op jit(solution)/shard_map/all_to_all | solution.py:163
  48.1 14.6 %dynamic_update_slice.38 = bf16[64,32,1024]{1,0,2:T(8,128)(2,1)} dynamic-update-slice(bf16[64,32,1024]{1,0,2:T(8,128)(2,1)} %copy.48, bf16[1,32,1024]{1,0,2:T(2,128)(2,1)S(1)} %copy.52, s32[]{:T(128)} %constant.159.clone.1, s32[]{:T(128)} %constant.159.clone.1, s32[]{:T(128)} %constant.159.clone.1) | dynamic-update-slice | bytes 131076 | tf_op jit(solution)/shard_map/while/body/eval_jaxpr/dynamic_update_slice | solution.py:149
  62.7 33.1 %gather_fusion.2 = bf16[144,32,128]{1,0,2:T(8,128)(2,1)} fusion(bf16[64,32,1024]{1,0,2:T(8,128)(2,1)} %dynamic_update_slice.38, s32[144]{0:T(256)S(1)} %bitcast.352), kind=kCustom, calls=%fused_computation.2 | custom fusion | bytes 2361024 | tf_op jit(solution)/shard_map/while/body/eval_jaxpr/vmap()/gather | solution.py:128
  95.8 7.6 %copy.55 = bf16[144,32,128]{2,1,0:T(8,128)(2,1)} copy(bf16[144,32,128]{1,0,2:T(8,128)(2,1)} %gather_fusion.2) | data formatting | bytes 2359296 | tf_op jit(solution)/shard_map/while/body/eval_jaxpr/vmap()/gather | solution.py:128
  103.3 6.1 %all-to-all-start.1 = ((bf16[8,6,3,32,128]{4,3,2,1,0:T(8,128)(2,1)}), bf16[8,6,3,32,128]{4,3,2,1,0:T(8,128)(2,1)}, u32[]{:S(2)}, u32[]{:S(2)}) async-start(bf16[8,6,3,32,128]{4,3,2,1,0:T(8,128)(2,1)} %bitcast.23), calls=%async_computation.1 | async-start | bytes 2359296 | tf_op jit(solution)/shard_map/while/body/eval_jaxpr/all_to_all | solution.py:173
  111.8 0.7 gather_fusion.1
  112.6 4.0 %fusion.23 = f32[1,32,1024]{2,1,0:T(8,128)S(1)} fusion(bf16[1,24,128,1024]{3,2,1,0:T(8,128)(2,1)} %param.12, bf16[24,32,128]{2,1,0:T(8,128)(2,1)S(1)} %gather_fusion.1, f32[32,1024]{1,0:T(8,128)S(1)} %copy-done.1, f32[6,32,1024]{2,1,0:T(8,128)S(1)} %copy-done.2, bf16[24]{0:T(256)(128)(2,1)S(1)} %fusion.185), kind=kOutput, calls=%fused_computation.16 | convolution fusion | flops 201883648 | bytes 7143472 | tf_op jit(solution)/shard_map/dot_general | solution.py:141
  117.3 0.8 slice.528
  118.0 0.8 fusion.129
  118.9 16.0 %all-to-all-done.1 = bf16[8,6,3,32,128]{4,3,2,1,0:T(8,128)(2,1)} async-done(((bf16[8,6,3,32,128]{4,3,2,1,0:T(8,128)(2,1)}), bf16[8,6,3,32,128]{4,3,2,1,0:T(8,128)(2,1)}, u32[]{:S(2)}, u32[]{:S(2)}) %all-to-all-start.1) | async-done | bytes 1179680 | tf_op jit(solution)/shard_map/while/body/eval_jaxpr/all_to_all | solution.py:173
  134.8 2.1 gather_fusion.3
  137.1 0.8 copy.56
  137.9 4.2 %fusion.2 = f32[192,1024]{1,0:T(8,128)S(1)} fusion(bf16[3072,1024]{1,0:T(8,128)(2,1)} %bitcast.351, bf16[24,8,24,128]{3,2,1,0:T(8,128)(2,1)S(1)} %bitcast.353), kind=kOutput, calls=%fused_computation.6 | convolution fusion | flops 1207959552 | bytes 8257536 | tf_op jit(solution)/shard_map/while/body/eval_jaxpr/dot_general | solution.py:141
  143.2 0.8 convolution_bitcast_fusion.5
  144.2 0.8 convolution_bitcast_fusion.4
  145.9 0.8 convolution_bitcast_fusion.3
  147.5 0.8 convolution_bitcast_fusion.2
  149.2 0.8 convolution_bitcast_fusion.1
  150.8 0.8 convolution_bitcast_fusion
  151.7 128.9 %all-reduce.4.cloned.1.call-done = (f32[1,128,32]{1,2,0:T(8,128)}, f32[1,128,32]{1,2,0:T(8,128)}, f32[1,128,32]{1,2,0:T(8,128)}, f32[1,128,32]{1,2,0:T(8,128)}, ...) async-done(((f32[1,128,32]{1,2,0:T(8,128)}, f32[1,128,32]{1,2,0:T(8,128)}, f32[1,128,32]{1,2,0:T(8,128)}, f32[1,128,32]{1,2,0:T(8,128)}, f32[1,128,32]{1,2,0:T(8,128)}, ...) | async-done | bytes 98320 | tf_op jit(solution)/shard_map/while/body/eval_jaxpr/psum | solution.py:158
  280.6 0.7 dynamic_update_slice.39
  281.4 0.7 constant_dynamic-update-slice_fusion.3
  282.1 0.7 constant_dynamic-update-slice_fusion.2
  282.8 0.7 constant_dynamic-update-slice_fusion.1
  283.5 0.7 constant_dynamic-update-slice_fusion
  (110 shorter events, 10.7 us)
Async XLA Ops:
  7.2 136.0 %copy-start = (bf16[128,1024]{1,0:T(8,128)(2,1)S(1)}, bf16[128,1024]{1,0:T(8,128)(2,1)}, u32[]{:S(2)}) copy-start(bf16[128,1024]{1,0:T(8,128)(2,1)} %param.13) | copy-start | bytes 786436
  39.9 7.6 %copy-start.2 = (f32[6,32,1024]{2,1,0:T(8,128)S(1)}, f32[6,32,1024]{2,1,0:T(8,128)}, u32[]{:S(2)}) copy-start(f32[6,32,1024]{2,1,0:T(8,128)} %param.9) | copy-start | bytes 2359300
  41.1 62.3 %all-to-all-start = ((bf16[8,1,3,32,128]{4,3,2,1,0:T(8,128)(2,1)}), bf16[8,1,3,32,128]{4,3,2,1,0:T(8,128)(2,1)S(1)}, u32[]{:S(2)}, u32[]{:S(2)}) async-start(bf16[8,1,3,32,128]{4,3,2,1,0:T(8,128)(2,1)} %bitcast.8), calls=%async_computation | async-start | bytes 393216 | tf_op jit(solution)/shard_map/all_to_all | solution.py:163
  47.7 68.9 %copy-start.4 = (f32[1,32,1024]{2,1,0:T(8,128)}, f32[1,32,1024]{2,1,0:T(8,128)S(1)}, u32[]{:S(2)}) copy-start(f32[1,32,1024]{2,1,0:T(8,128)S(1)} %get-tuple-element.77) | copy-start | bytes 393220
  47.7 68.9 %copy-start.6 = (f32[1,32,1024]{2,1,0:T(8,128)}, f32[1,32,1024]{2,1,0:T(8,128)S(1)}, u32[]{:S(2)}) copy-start(f32[1,32,1024]{2,1,0:T(8,128)S(1)} %get-tuple-element.78) | copy-start | bytes 393220
  103.3 6.2 %copy-start.15 = (s32[32]{0:T(128)S(1)}, s32[32]{0:T(128)}, u32[]{:S(2)}) copy-start(s32[32]{0:T(128)} %param.17) | copy-start | bytes 388
  103.3 6.8 %copy-start.14 = (s32[32,24]{0,1:T(8,128)S(1)}, s32[32,24]{0,1:T(8,128)}, u32[]{:S(2)}) copy-start(s32[32,24]{0,1:T(8,128)} %param.14) | copy-start | bytes 9220
  103.3 31.5 %all-to-all-start.1 = ((bf16[8,6,3,32,128]{4,3,2,1,0:T(8,128)(2,1)}), bf16[8,6,3,32,128]{4,3,2,1,0:T(8,128)(2,1)}, u32[]{:S(2)}, u32[]{:S(2)}) async-start(bf16[8,6,3,32,128]{4,3,2,1,0:T(8,128)(2,1)} %bitcast.23), calls=%async_computation.1 | async-start | bytes 2359296 | tf_op jit(solution)/shard_map/while/body/eval_jaxpr/all_to_all | solution.py:173
  109.5 3.1 %copy-start.1 = (f32[32,1024]{1,0:T(8,128)S(1)}, f32[32,1024]{1,0:T(8,128)}, u32[]{:S(2)}) copy-start(f32[32,1024]{1,0:T(8,128)} %param.10) | copy-start | bytes 393220
  109.5 171.1 %all-reduce.4.cloned.1.call-start = ((), (), s32[]{:S(2)}) async-start(), calls=%async_computation.2 | async-start | bytes 196608 | tf_op jit(solution)/shard_map/while/body/eval_jaxpr/psum | solution.py:158
  116.6 0.7 copy-start.8
  137.9 4.4 %copy-start.3 = (f32[3,32,1024]{2,1,0:T(8,128)S(1)}, f32[3,32,1024]{2,1,0:T(8,128)}, u32[]{:S(2)}) copy-start(f32[3,32,1024]{2,1,0:T(8,128)} %slice.528) | copy-start | bytes 1179652
  137.9 4.4 %copy-start.5 = (f32[1,32,1024]{2,1,0:T(8,128)S(1)}, f32[1,32,1024]{2,1,0:T(8,128)}, u32[]{:S(2)}) copy-start(f32[1,32,1024]{2,1,0:T(8,128)} %copy-done.4) | copy-start | bytes 393220
  137.9 4.4 %copy-start.7 = (f32[1,32,1024]{2,1,0:T(8,128)S(1)}, f32[1,32,1024]{2,1,0:T(8,128)}, u32[]{:S(2)}) copy-start(f32[1,32,1024]{2,1,0:T(8,128)} %copy-done.6) | copy-start | bytes 393220
  137.9 4.4 %copy-start.9 = (f32[1,32,1024]{2,1,0:T(8,128)S(1)}, f32[1,32,1024]{2,1,0:T(8,128)}, u32[]{:S(2)}) copy-start(f32[1,32,1024]{2,1,0:T(8,128)} %copy-done.8) | copy-start | bytes 393220
  137.9 4.4 %copy-start.11 = (f32[1,32,1024]{2,1,0:T(8,128)S(1)}, f32[1,32,1024]{2,1,0:T(8,128)}, u32[]{:S(2)}) copy-start(f32[1,32,1024]{2,1,0:T(8,128)} %get-tuple-element.74) | copy-start | bytes 393220
  137.9 4.4 %copy-start.12 = (f32[1,32,1024]{2,1,0:T(8,128)S(1)}, f32[1,32,1024]{2,1,0:T(8,128)}, u32[]{:S(2)}) copy-start(f32[1,32,1024]{2,1,0:T(8,128)} %get-tuple-element.75) | copy-start | bytes 393220
  150.8 134.1 %copy-start.10 = (f32[6,32,1024]{2,1,0:T(8,128)}, f32[6,32,1024]{2,1,0:T(8,128)S(1)}, u32[]{:S(2)}) copy-start(f32[6,32,1024]{2,1,0:T(8,128)S(1)} %fusion.37) | copy-start | bytes 2359300
  285.0 0.6 copy-start.13
Sparse Core Ops, SparseCore 0:
  151.8 128.7 all-reduce.3
where the time goes:
time: 294 us; the launch traced here: 292 us
  waiting for transfers between devices  145 us (49%)
  local copies, waits for them, and re-layouts  100 us (34%)
  between operations  14.7 us (5%)
  matrix products  13.1 us (4%)
  starting transfers between devices  12.2 us (4%)
  other arithmetic  7.27 us (2%)
    psum x1, waiting for transfers between devices, record(): local_sum = lax.psum(local_sum, ('grp', 'node'))  129 us
    gather x4, local copies, waits for them, and re-layouts, cut_piece(): lax.dynamic_slice(cycle, (slot_id, zero_index, start_id), (1, replicas, p...  47.3 us
    unnamed x36, local copies, waits for them, and re-layouts  26.6 us
    all_to_all x1, waiting for transfers between devices, one_batch(): lax.all_to_all(pack(cycle, in_times), 'grp', split_axis=0, concat_axis=0,...  16 us
    dynamic_update_slice x1, local copies, waits for them, and re-layouts, store_fire(): lax.dynamic_update_slice(cycle, spike_density_result[None], (jnp.mod(step...  14.6 us
    dot_general x2, matrix products, unpack(): jnp.dot(flattened, tile_stack, preferred_element_type=jnp.float32)  8.29 us
    all_to_all x1, starting transfers between devices, one_batch(): lax.all_to_all(pack(cycle, in_times), 'grp', split_axis=0, concat_axis=0,...  6.14 us
    all_to_all x1, starting transfers between devices, body(): lax.all_to_all(pack(history, start_times), 'grp', split_axis=0, concat_ax...  6.07 us
  transfers between devices with their start and end apart: 3, of which 2 were waited for; matrix products, arithmetic and copies ran while one was open for 22% of the time, Pallas kernels for 0%

commit v1 on v0

--- a/solution.py
+++ b/solution.py
@@ -15,6 +15,11 @@
 fire_slope = 0.56
 global_scaling_factor = 0.5
 dt_step = 0.5
+
+
+def add_all(shard, name):
+    blocks = lax.all_gather(shard, name)
+    return jnp.sum(blocks, axis=0)
 
 
 def sigmoid_spike_density(somatic_charge_level):
@@ -155,7 +160,7 @@
         local_sum = lax.dot_general(
             lead_field, potential, (((1,), (1,)), ((), ())), preferred_element_type=jnp.float32
         )
-        local_sum = lax.psum(local_sum, ("grp", "node"))
+        local_sum = add_all(local_sum, ("grp", "node"))
         return lax.dynamic_update_slice(sensors, local_sum[None], (step_id, zero_index, zero_index))
 
     start_times = jnp.zeros((1,), jnp.int32)

time: 294 us -> 384 us (1.31)
  the two profiles are of different devices: /device:TPU:8 before, /device:TPU:0 now
where the time goes in v1:
time: 384 us; the launch traced here: 383 us
  blocking collectives  235 us (61%)
  local copies, waits for them, and re-layouts  97.8 us (25%)
  waiting for transfers between devices  18.9 us (5%)
  starting transfers between devices  13 us (3%)
  matrix products  9.38 us (2%)
  other arithmetic  7.69 us (2%)
    all_gather x6, blocking collectives, add_all(): blocks = lax.all_gather(shard, name)  235 us
    gather x4, local copies, waits for them, and re-layouts, cut_piece(): lax.dynamic_slice(cycle, (slot_id, zero_index, start_id), (1, replicas, p...  47.9 us
    unnamed x44, local copies, waits for them, and re-layouts  27.9 us
    all_to_all x1, waiting for transfers between devices, one_batch(): lax.all_to_all(pack(cycle, in_times), 'grp', split_axis=0, concat_axis=0,...  18.9 us
    dynamic_update_slice x1, local copies, waits for them, and re-layouts, store_fire(): lax.dynamic_update_slice(cycle, spike_density_result[None], (jnp.mod(step...  14.6 us
    dot_general x2, matrix products, unpack(): jnp.dot(flattened, tile_stack, preferred_element_type=jnp.float32)  8.29 us
  transfers between devices with their start and end apart: 2, of which 1 were waited for; matrix products, arithmetic and copies ran while one was open for 17% of the time, Pallas kernels for 0%

profile of v1, /device:TPU:0, one launch (start us, length us, event | category | flops | bytes accessed | tf_op | source)
XLA Modules:
  0.0 382.9 jit_solution(7776598898308544330)
XLA Ops:
  0.7 0.8 reshape.515
  1.4 0.8 copy.46
  2.2 0.8 copy.44
  3.0 0.8 copy.43
  4.8 23.1 %copy.48 = bf16[64,32,1024]{1,0,2:T(8,128)(2,1)} copy(bf16[64,32,1024]{2,1,0:T(8,128)(2,1)} %param.11) | data formatting | bytes 8388608 | tf_op args[2]
  27.9 5.8 %gather_fusion = bf16[24,32,128]{1,0,2:T(8,128)(2,1)S(1)} fusion(bf16[64,32,1024]{1,0,2:T(8,128)(2,1)} %copy.48, s32[24]{0:T(128)S(1)} %fusion.184), kind=kCustom, calls=%fused_computation | custom fusion | bytes 393504 | tf_op jit(solution)/shard_map/vmap()/gather | solution.py:133
  33.7 1.1 copy.49
  34.8 7.2 %all-to-all-start = ((bf16[8,1,3,32,128]{4,3,2,1,0:T(8,128)(2,1)}), bf16[8,1,3,32,128]{4,3,2,1,0:T(8,128)(2,1)S(1)}, u32[]{:S(2)}, u32[]{:S(2)}) async-start(bf16[8,1,3,32,128]{4,3,2,1,0:T(8,128)(2,1)} %bitcast.8), calls=%async_computation | async-start | bytes 393216 | tf_op jit(solution)/shard_map/all_to_all | solution.py:168
  43.0 14.6 %dynamic_update_slice.38 = bf16[64,32,1024]{1,0,2:T(8,128)(2,1)} dynamic-update-slice(bf16[64,32,1024]{1,0,2:T(8,128)(2,1)} %copy.48, bf16[1,32,1024]{1,0,2:T(2,128)(2,1)S(1)} %copy.52, s32[]{:T(128)} %constant.161.clone.1, s32[]{:T(128)} %constant.161.clone.1, s32[]{:T(128)} %constant.161.clone.1) | dynamic-update-slice | bytes 131076 | tf_op jit(solution)/shard_map/while/body/eval_jaxpr/dynamic_update_slice | solution.py:154
  57.6 33.4 %gather_fusion.2 = bf16[144,32,128]{1,0,2:T(8,128)(2,1)} fusion(bf16[64,32,1024]{1,0,2:T(8,128)(2,1)} %dynamic_update_slice.38, s32[144]{0:T(256)S(1)} %bitcast.381), kind=kCustom, calls=%fused_computation.2 | custom fusion | bytes 2361024 | tf_op jit(solution)/shard_map/while/body/eval_jaxpr/vmap()/gather | solution.py:133
  91.0 7.6 %copy.55 = bf16[144,32,128]{2,1,0:T(8,128)(2,1)} copy(bf16[144,32,128]{1,0,2:T(8,128)(2,1)} %gather_fusion.2) | data formatting | bytes 2359296 | tf_op jit(solution)/shard_map/while/body/eval_jaxpr/vmap()/gather | solution.py:133
  98.6 5.8 %all-to-all-start.1 = ((bf16[8,6,3,32,128]{4,3,2,1,0:T(8,128)(2,1)}), bf16[8,6,3,32,128]{4,3,2,1,0:T(8,128)(2,1)}, u32[]{:S(2)}, u32[]{:S(2)}) async-start(bf16[8,6,3,32,128]{4,3,2,1,0:T(8,128)(2,1)} %bitcast.23), calls=%async_computation.1 | async-start | bytes 2359296 | tf_op jit(solution)/shard_map/while/body/eval_jaxpr/all_to_all | solution.py:178
  104.4 0.6 dynamic_slice.27
  105.2 0.7 fusion.185
  105.9 0.7 iota_compare_fusion.3
  106.7 0.7 gather_fusion.1
  107.5 4.0 %fusion.23 = f32[1,32,1024]{2,1,0:T(8,128)S(1)} fusion(bf16[1,24,128,1024]{3,2,1,0:T(8,128)(2,1)} %param.12, bf16[24,32,128]{2,1,0:T(8,128)(2,1)S(1)} %gather_fusion.1, f32[32,1024]{1,0:T(8,128)S(1)} %copy-done.1, f32[6,32,1024]{2,1,0:T(8,128)S(1)} %copy-done.2, bf16[24]{0:T(256)(128)(2,1)S(1)} %fusion.185), kind=kOutput, calls=%fused_computation.16 | convolution fusion | flops 201883648 | bytes 7143472 | tf_op jit(solution)/shard_map/dot_general | solution.py:146
  111.7 0.5 copy-done.9
  112.2 0.8 slice.528
  112.9 0.8 fusion.129
  113.8 18.9 %all-to-all-done.1 = bf16[8,6,3,32,128]{4,3,2,1,0:T(8,128)(2,1)} async-done(((bf16[8,6,3,32,128]{4,3,2,1,0:T(8,128)(2,1)}), bf16[8,6,3,32,128]{4,3,2,1,0:T(8,128)(2,1)}, u32[]{:S(2)}, u32[]{:S(2)}) %all-to-all-start.1) | async-done | bytes 1179680 | tf_op jit(solution)/shard_map/while/body/eval_jaxpr/all_to_all | solution.py:178
  132.7 2.1 gather_fusion.3
  135.0 0.8 copy.56
  135.8 4.2 %fusion.2 = f32[192,1024]{1,0:T(8,128)S(1)} fusion(bf16[3072,1024]{1,0:T(8,128)(2,1)} %bitcast.380, bf16[24,8,24,128]{3,2,1,0:T(8,128)(2,1)S(1)} %bitcast.388), kind=kOutput, calls=%fused_computation.6 | convolution fusion | flops 1207959552 | bytes 8257536 | tf_op jit(solution)/shard_map/while/body/eval_jaxpr/dot_general | solution.py:146
  145.4 0.7 copy-done.3
  146.1 41.6 %all-gather = f32[4096,32]{0,1:T(8,128)S(1)} all-gather(f32[128,32]{0,1:T(8,128)S(1)} %convolution_bitcast_fusion.5), channel_id=2, replica_groups=mesh['grp'=8,'node'=4] {'grp','node'}, dimensions={0}, use_global_device_ids=true | all-gather | bytes 540672 | tf_op jit(solution)/shard_map/while/body/eval_jaxpr/all_gather | solution.py:21
  187.9 38.1 %all-gather.1 = f32[4096,32]{0,1:T(8,128)S(1)} all-gather(f32[128,32]{0,1:T(8,128)S(1)} %convolution_bitcast_fusion.4), channel_id=3, replica_groups=mesh['grp'=8,'node'=4] {'grp','node'}, dimensions={0}, use_global_device_ids=true | all-gather | bytes 540672 | tf_op jit(solution)/shard_map/while/body/eval_jaxpr/all_gather | solution.py:21
  226.1 39.4 %all-gather.2 = f32[4096,32]{0,1:T(8,128)S(1)} all-gather(f32[128,32]{0,1:T(8,128)S(1)} %convolution_bitcast_fusion.3), channel_id=4, replica_groups=mesh['grp'=8,'node'=4] {'grp','node'}, dimensions={0}, use_global_device_ids=true | all-gather | bytes 540672 | tf_op jit(solution)/shard_map/while/body/eval_jaxpr/all_gather | solution.py:21
  265.6 38.1 %all-gather.3 = f32[4096,32]{0,1:T(8,128)S(1)} all-gather(f32[128,32]{0,1:T(8,128)S(1)} %convolution_bitcast_fusion.2), channel_id=5, replica_groups=mesh['grp'=8,'node'=4] {'grp','node'}, dimensions={0}, use_global_device_ids=true | all-gather | bytes 540672 | tf_op jit(solution)/shard_map/while/body/eval_jaxpr/all_gather | solution.py:21
  303.9 39.5 %all-gather.4 = f32[4096,32]{0,1:T(8,128)S(1)} all-gather(f32[128,32]{0,1:T(8,128)S(1)} %convolution_bitcast_fusion.1), channel_id=6, replica_groups=mesh['grp'=8,'node'=4] {'grp','node'}, dimensions={0}, use_global_device_ids=true | all-gather | bytes 540672 | tf_op jit(solution)/shard_map/while/body/eval_jaxpr/all_gather | solution.py:21
  344.0 38.1 %all-gather.5 = f32[4096,32]{0,1:T(8,128)S(1)} all-gather(f32[128,32]{0,1:T(8,128)S(1)} %convolution_bitcast_fusion), channel_id=7, replica_groups=mesh['grp'=8,'node'=4] {'grp','node'}, dimensions={0}, use_global_device_ids=true | all-gather | bytes 540672 | tf_op jit(solution)/shard_map/while/body/eval_jaxpr/all_gather | solution.py:21
  382.3 0.6 copy-done.14
  (128 shorter events, 9.0 us)
Async XLA Ops:
  0.6 140.4 %copy-start = (bf16[128,1024]{1,0:T(8,128)(2,1)S(1)}, bf16[128,1024]{1,0:T(8,128)(2,1)}, u32[]{:S(2)}) copy-start(bf16[128,1024]{1,0:T(8,128)(2,1)} %param.13) | copy-start | bytes 786436
  33.7 8.8 %copy-start.2 = (f32[6,32,1024]{2,1,0:T(8,128)S(1)}, f32[6,32,1024]{2,1,0:T(8,128)}, u32[]{:S(2)}) copy-start(f32[6,32,1024]{2,1,0:T(8,128)} %param.9) | copy-start | bytes 2359300
  34.8 63.8 %all-to-all-start = ((bf16[8,1,3,32,128]{4,3,2,1,0:T(8,128)(2,1)}), bf16[8,1,3,32,128]{4,3,2,1,0:T(8,128)(2,1)S(1)}, u32[]{:S(2)}, u32[]{:S(2)}) async-start(bf16[8,1,3,32,128]{4,3,2,1,0:T(8,128)(2,1)} %bitcast.8), calls=%async_computation | async-start | bytes 393216 | tf_op jit(solution)/shard_map/all_to_all | solution.py:168
  42.6 68.9 %copy-start.5 = (f32[1,32,1024]{2,1,0:T(8,128)}, f32[1,32,1024]{2,1,0:T(8,128)S(1)}, u32[]{:S(2)}) copy-start(f32[1,32,1024]{2,1,0:T(8,128)S(1)} %get-tuple-element.71) | copy-start | bytes 393220
  42.6 68.9 %copy-start.7 = (f32[1,32,1024]{2,1,0:T(8,128)}, f32[1,32,1024]{2,1,0:T(8,128)S(1)}, u32[]{:S(2)}) copy-start(f32[1,32,1024]{2,1,0:T(8,128)S(1)} %get-tuple-element.72) | copy-start | bytes 393220
  98.6 5.8 %copy-start.16 = (s32[32]{0:T(128)S(1)}, s32[32]{0:T(128)}, u32[]{:S(2)}) copy-start(s32[32]{0:T(128)} %param.17) | copy-start | bytes 388
  98.6 6.4 %copy-start.15 = (s32[32,24]{0,1:T(8,128)S(1)}, s32[32,24]{0,1:T(8,128)}, u32[]{:S(2)}) copy-start(s32[32,24]{0,1:T(8,128)} %param.14) | copy-start | bytes 9220
  98.6 34.1 %all-to-all-start.1 = ((bf16[8,6,3,32,128]{4,3,2,1,0:T(8,128)(2,1)}), bf16[8,6,3,32,128]{4,3,2,1,0:T(8,128)(2,1)}, u32[]{:S(2)}, u32[]{:S(2)}) async-start(bf16[8,6,3,32,128]{4,3,2,1,0:T(8,128)(2,1)} %bitcast.23), calls=%async_computation.1 | async-start | bytes 2359296 | tf_op jit(solution)/shard_map/while/body/eval_jaxpr/all_to_all | solution.py:178
  104.4 3.1 copy-start.1
  111.5 0.7 copy-start.9
  135.7 4.4 %copy-start.4 = (f32[3,32,1024]{2,1,0:T(8,128)S(1)}, f32[3,32,1024]{2,1,0:T(8,128)}, u32[]{:S(2)}) copy-start(f32[3,32,1024]{2,1,0:T(8,128)} %slice.528) | copy-start | bytes 1179652
  135.7 4.4 %copy-start.6 = (f32[1,32,1024]{2,1,0:T(8,128)S(1)}, f32[1,32,1024]{2,1,0:T(8,128)}, u32[]{:S(2)}) copy-start(f32[1,32,1024]{2,1,0:T(8,128)} %copy-done.5) | copy-start | bytes 393220
  135.7 4.4 %copy-start.8 = (f32[1,32,1024]{2,1,0:T(8,128)S(1)}, f32[1,32,1024]{2,1,0:T(8,128)}, u32[]{:S(2)}) copy-start(f32[1,32,1024]{2,1,0:T(8,128)} %copy-done.7) | copy-start | bytes 393220
  135.8 4.4 %copy-start.10 = (f32[1,32,1024]{2,1,0:T(8,128)S(1)}, f32[1,32,1024]{2,1,0:T(8,128)}, u32[]{:S(2)}) copy-start(f32[1,32,1024]{2,1,0:T(8,128)} %copy-done.9) | copy-start | bytes 393220
  135.8 4.4 %copy-start.12 = (f32[1,32,1024]{2,1,0:T(8,128)S(1)}, f32[1,32,1024]{2,1,0:T(8,128)}, u32[]{:S(2)}) copy-start(f32[1,32,1024]{2,1,0:T(8,128)} %get-tuple-element.68) | copy-start | bytes 393220
  135.8 4.4 %copy-start.13 = (f32[1,32,1024]{2,1,0:T(8,128)S(1)}, f32[1,32,1024]{2,1,0:T(8,128)}, u32[]{:S(2)}) copy-start(f32[1,32,1024]{2,1,0:T(8,128)} %get-tuple-element.69) | copy-start | bytes 393220
  145.2 0.9 copy-start.3
  303.9 39.7 %slice-start = ((f32[6,32,1024]{2,1,0:T(8,128)}), f32[3,32,1024]{2,1,0:T(8,128)S(1)}, s32[]{:S(2)}) async-start(f32[6,32,1024]{2,1,0:T(8,128)} %copy-done.3), calls=%async_computation.2 | async-start | bytes 786432 | tf_op jit(solution)/shard_map/while/body/eval_jaxpr/slice | solution.py:69
  343.8 38.4 %copy-start.11 = (f32[6,32,1024]{2,1,0:T(8,128)}, f32[6,32,1024]{2,1,0:T(8,128)S(1)}, u32[]{:S(2)}) copy-start(f32[6,32,1024]{2,1,0:T(8,128)S(1)} %fusion.37) | copy-start | bytes 2359300
  382.3 0.6 copy-start.14
